TPU v7x, 128 devices: a whole 4x4x4 slice. The times are simulated.
128 devices in a mesh: tok: 8 (over z_lo, x), row: 4 (over z_hi, core), col: 4 (over y).
Axes of the slice: x: 4, y: 4, z: 4 (z_hi: 2, z_lo: 2; z = z_hi * 2 + z_lo), core: 2. Of those that a mesh axis runs over, the one named last changes fastest.
Arguments:
- activations: bfloat16 [2, 1024, 28672], P(None, 'tok', ('row', 'col')), may hold values from -0.1875 to 0.1875
- weights: bfloat16 [2, 28672, 8192], P(None, ('row', 'col'), 'tok'), may hold values from -6 to 6
Outputs:
- solved: float32 [256, 8192], P('row', ('tok', 'col'))
- correction: bfloat16 [28672, 8192], P(('row', 'col'), 'tok')
All inputs are finite; a program needn't handle non-finite values.
Results may differ from a plain program's by a relative error of at most 0.0073.
Values may be sent and summed in bfloat16 or wider, within the bound.
A program may use at most 64 MiB of HBM per device.

v0:
```python
import jax
import jax.numpy as jnp
from jax import lax
from jax.sharding import PartitionSpec as P

PANEL = 256


def broadcast(array, axis, root):
    return lax.dynamic_index_in_dim(lax.all_gather(array, axis), root, 0, keepdims=False)


def in_blocks(array, dim, peers):
    lengths = array.shape
    tiles = array.reshape(*lengths[:dim], peers, lengths[dim] // peers, *lengths[dim + 1 :])
    return jnp.moveaxis(tiles, dim, 0)


def summed_on_arrival(array, axis, dim):
    peers = lax.axis_size(axis)
    tiles = lax.all_to_all(in_blocks(array, dim, peers), axis, 0, 0, tiled=True)
    return jnp.sum(tiles, axis=0)


def joined_along(tiles, dim):
    tiles = jnp.moveaxis(tiles, 0, dim)
    lengths = tiles.shape
    return tiles.reshape(*lengths[:dim], lengths[dim] * lengths[dim + 1], *lengths[dim + 2 :])


def from_everyone(array, axis):
    peers = lax.axis_size(axis)
    return lax.all_to_all(
        jnp.broadcast_to(array[None], (peers, *array.shape)), axis, 0, 0, tiled=True
    )


def gather_directly(array, axis, dim):
    return joined_along(from_everyone(array, axis), dim)


def body(activations, weights):
    row_count = lax.axis_size("row")
    col_count = lax.axis_size("col")
    rows_here = activations.shape[2]
    panel_width = PANEL
    block_rows = panel_width // row_count
    out_here = weights.shape[2]
    block_cols = out_here // col_count
    first_row = lax.axis_index(("row", "col")) * rows_here
    panel_tokens = broadcast(activations[:, :, :panel_width], ("row", "col"), 0)
    partial_value = jnp.einsum(
        "mti,mtp->mip", activations, panel_tokens, preferred_element_type=jnp.float32
    )
    gram_sums = lax.psum(partial_value, "tok")
    row_ids = first_row + jnp.arange(rows_here, dtype=jnp.int32)[:, None]
    col_ids = jnp.arange(panel_width, dtype=jnp.int32)[None, :]
    on_diagonal = row_ids == col_ids
    regular = gram_sums * jnp.where(on_diagonal, 1.0, 0.9).astype(jnp.float32)[None]
    regular_bf16 = regular.astype(jnp.bfloat16)
    summed = regular[0] + regular[1]
    offset = jnp.int32(0)
    outputs = []
    for position in range(block_rows * lax.axis_size(("row", "col")) // block_rows):
        block_id = offset // block_rows + position
        tile_row = block_id // col_count
        tile_col = block_id % col_count
        gram_part = lax.dynamic_slice_in_dim(regular_bf16, tile_row * block_rows, block_rows, 2)
        weight_part = lax.dynamic_slice_in_dim(weights, tile_col * block_cols, block_cols, 2)
        outputs.append(
            jnp.einsum("mip,mio->po", gram_part, weight_part, preferred_element_type=jnp.float32)
        )
    right_block = summed_on_arrival(jnp.concatenate(outputs, axis=0), ("row", "col"), 0)
    diagonal_part = broadcast(summed[:panel_width], ("row", "col"), 0)
    factor = jnp.linalg.cholesky(diagonal_part)
    panel_factor = lax.linalg.triangular_solve(
        factor, summed, left_side=False, lower=True, transpose_a=True
    )
    row_index = lax.axis_index("row")
    whole_right = gather_directly(right_block, "row", 0)
    whole_solved = lax.linalg.triangular_solve(factor, whole_right, left_side=True, lower=True)
    solved = lax.dynamic_slice_in_dim(whole_solved, row_index * block_rows, block_rows, 0)
    solved_columns = lax.all_gather(solved, "col", axis=1, tiled=True)
    correction = jnp.dot(
        panel_factor,
        lax.all_gather(solved_columns, "row", axis=0, tiled=True),
        precision=lax.Precision.HIGHEST,
        preferred_element_type=jnp.float32,
    )
    return (solved, correction.astype(jnp.bfloat16))


def solution(mesh):
    in_specs = (P(None, "tok", ("row", "col")), P(None, ("row", "col"), "tok"))
    out_specs = (P("row", ("tok", "col")), P(("row", "col"), "tok"))
    return jax.shard_map(body, mesh=mesh, in_specs=in_specs, out_specs=out_specs, check_vma=False)
```

profile of v0, /device:TPU:1, one launch (start us, length us, event | category | flops | bytes accessed | tf_op | source)
XLA Modules:
  0.0 338.8 jit_solution(6505781074480112813)
XLA Ops:
  7.2 1.6 slice.77
  8.9 54.1 %all-gather.9.cloned.1.call-done = bf16[32,128,256]{2,1,0:T(8,128)(2,1)} async-done(((bf16[2,128,256]{2,1,0:T(8,128)(2,1)}), bf16[32,128,256]{2,1,0:T(8,128)(2,1)}) %all-gather.9.cloned.1.call-update) | async-done | bytes 2097168 | tf_op jit(solution)/shard_map/all_gather | solution.py:10
  62.9 3.7 %fusion.151 = f32[2,1792,256]{2,1,0:T(8,128)} fusion(bf16[2,128,1792]{2,1,0:T(8,128)(2,1)} %param.2, bf16[32,128,256]{2,1,0:T(8,128)(2,1)} %all-gather.9.cloned.1.call-done), kind=kOutput, calls=%fused_computation.101 | convolution fusion | flops 234881024 | bytes 4718592 | tf_op jit(solution)/shard_map/mti,mtp->mip/dot_general | solution.py:52
  67.0 94.8 %all-reduce.3.cloned.1.call-done = f32[2,1792,256]{2,1,0:T(8,128)} async-done(((f32[2,1792,256]{2,1,0:T(8,128)}), f32[2,1792,256]{2,1,0:T(8,128)}) %all-reduce.3.cloned.1.call-update) | async-done | bytes 3670032 | tf_op jit(solution)/shard_map/psum | solution.py:55
  161.8 3.8 %fusion.163 = (bf16[2,1792,256]{2,1,0:T(8,128)(2,1)}, f32[2,1792,256]{2,1,0:T(8,128)S(1)}) fusion(f32[2,1792,256]{2,1,0:T(8,128)} %all-reduce.3.cloned.1.call-done, f32[1792,256]{1,0:T(8,128)S(1)} %fusion.3), kind=kLoop, calls=%fused_computation.126 | loop fusion | flops 1835008 | bytes 11010048 | tf_op jit(solution)/shard_map/convert_element_type | solution.py:60
  165.8 1.6 copy-done
  168.4 2.1 fusion.39
  170.5 2.0 fusion.63
  172.5 2.1 fusion.87
  174.6 2.0 fusion.111
  176.6 2.3 fusion.45
  185.6 0.8 fusion.129
  186.3 25.9 %all_to_all.10 = f32[16,64,256]{2,1,0:T(8,128)S(1)} all-to-all(f32[16,64,256]{2,1,0:T(8,128)S(1)} %bitcast.111), channel_id=1, replica_groups=mesh['tok'=8,'row'=4,'col'=4] {'row','col'}, dimensions={0} | all-to-all | bytes 2097152 | tf_op jit(solution)/shard_map/all_to_all | solution.py:21
  213.0 5.3 %all-to-all-start.1 = ((f32[4,64,256]{2,1,0:T(8,128)}), f32[4,64,256]{2,1,0:T(8,128)S(1)}, u32[]{:S(2)}, u32[]{:S(2)}) async-start(f32[4,64,256]{2,1,0:T(8,128)} %broadcast_in_dim.21), calls=%async_computation.1 | async-start | bytes 524288 | tf_op jit(solution)/shard_map/all_to_all | solution.py:33
  218.3 6.5 %all-to-all-done.1 = f32[4,64,256]{2,1,0:T(8,128)S(1)} async-done(((f32[4,64,256]{2,1,0:T(8,128)}), f32[4,64,256]{2,1,0:T(8,128)S(1)}, u32[]{:S(2)}, u32[]{:S(2)}) %all-to-all-start.1) | async-done | bytes 262176 | tf_op jit(solution)/shard_map/all_to_all | solution.py:33
  224.9 5.5 %all-gather.5.cloned.1.call-done = f32[16,256,256]{2,1,0:T(8,128)} async-done(((f32[1,256,256]{2,1,0:T(8,128)}), f32[16,256,256]{2,1,0:T(8,128)}) %all-gather.5.cloned.1.call-update) | async-done | bytes 4194320 | tf_op jit(solution)/shard_map/all_gather | solution.py:10
  230.4 1.0 dynamic_slice.70
  231.5 1.0 fusion.150
  232.5 11.7 %cholesky.50 = f32[128,128]{1,0:T(8,128)S(1)} custom-call(f32[128,128]{1,0:T(8,128)S(1)} %cholesky.118), custom_call_target="Cholesky" | custom-call | tf_op jit(solution)/shard_map/jit(cholesky)/cholesky | solution.py:75
  244.2 9.8 %custom-call.16 = f32[1,128,128]{1,2,0:T(8,128)S(1)} custom-call(f32[1,128,128]{2,1,0:T(8,128)S(1)} %get-tuple-element.27), custom_call_target="InvertDiagBlocksLowerTriangular" | custom-call | tf_op jit(solution)/shard_map/jit(cholesky)/cholesky | solution.py:75
  254.5 11.7 %cholesky.105 = f32[128,128]{1,0:T(8,128)S(1)} custom-call(f32[128,128]{1,0:T(8,128)S(1)} %convolution_subtract_fusion.2), custom_call_target="Cholesky" | custom-call | tf_op jit(solution)/shard_map/jit(cholesky)/cholesky | solution.py:75
  268.4 4.2 %while.1 = (s32[]{:T(128)}, f32[256,256]{1,0:T(8,128)S(1)}, s32[2,2]{1,0:T(2,128)S(1)}, f32[2,128,128]{2,1,0:T(8,128)S(1)}, s32[]{:T(128)}) while((s32[]{:T(128)}, f32[256,256]{1,0:T(8,128)S(1)}, s32[2,2]{1,0:T(2,128)S(1)}, f32[2,128,128]{2,1,0:T(8,128)S(1)}, s32[]{:T(128)}) %tuple.29), condition=%wide.while_cond, body=%wide.while_body.sunk | while | flops 2 | bytes 131181 | solution.py:81
  269.2 1.3 bitcast_dynamic-update-slice_fusion.2
  271.2 1.3 bitcast_dynamic-update-slice_fusion.2
  272.6 19.7 %custom-call.17 = f32[2,128,128]{1,2,0:T(8,128)S(1)} custom-call(f32[2,128,128]{2,1,0:T(8,128)S(1)} %get-tuple-element.9), custom_call_target="InvertDiagBlocksLowerTriangular" | custom-call | tf_op jit(solution)/shard_map/triangular_solve | solution.py:81
  293.2 10.1 %all_gather.19 = f32[64,1024]{1,0:T(8,128)} all-gather(f32[64,256]{1,0:T(8,128)S(1)} %fusion.153), channel_id=1, replica_groups=mesh['tok'=8,'row'=4,'col'=4] {'col'}, dimensions={1}, use_global_device_ids=true | all-gather | bytes 327680 | tf_op jit(solution)/shard_map/all_gather | solution.py:83
  303.4 2.3 fusion.175
  305.7 1.0 fusion.132
  306.6 1.6 convolution_subtract_fusion
  308.2 1.0 fusion.158
  309.2 14.3 %all-gather.7.cloned.1.call-done = f32[256,1024]{1,0:T(8,128)} async-done(((f32[64,1024]{1,0:T(8,128)}), f32[256,1024]{1,0:T(8,128)}) %all-gather.7.cloned.1.call-update) | async-done | bytes 1048592 | tf_op jit(solution)/shard_map/all_gather | solution.py:86
  323.5 8.7 %convolution_convert_fusion = bf16[1792,1024]{1,0:T(8,128)(2,1)} fusion(f32[256,1024]{1,0:T(8,128)} %all-gather.7.cloned.1.call-done, f32[1792,128]{0,1:T(8,128)S(1)} %fusion.158, f32[1792,128]{0,1:T(8,128)S(1)} %fusion.132), kind=kOutput, calls=%fused_computation.2 | convolution fusion | flops 5639438336 | bytes 6553600 | tf_op jit(solution)/shard_map/dot_general | solution.py:84
  (55 shorter events, 12.7 us)
Async XLA Ops:
  7.2 55.7 %all-gather.9.cloned.1.call-start = ((), (), s32[]{:S(2)}) async-start(), calls=%async_computation.5 | async-start | bytes 2228224 | tf_op jit(solution)/shard_map/all_gather | solution.py:10
  8.8 153.0 %all-reduce.3.cloned.1.call-start = ((), (), s32[]{:S(2)}) async-start(), calls=%async_computation.2 | async-start | bytes 7340032 | tf_op jit(solution)/shard_map/psum | solution.py:55
  66.6 163.7 %all-gather.5.cloned.1.call-start = ((), (), s32[]{:S(2)}) async-start(), calls=%async_computation.3 | async-start | bytes 4456448 | tf_op jit(solution)/shard_map/all_gather | solution.py:10
  165.6 1.9 copy-start
  165.6 2.8 copy-start.1
  168.4 10.5 %slice-start = ((s8[7340032]{0:T(1024)(128)(4,1)}), s8[4194304]{0:T(1024)(128)(4,1)S(1)}, s32[]{:S(2)}) async-start(s8[7340032]{0:T(1024)(128)(4,1)} %bitcast.114), calls=%async_computation.6 | async-start | bytes 8388608
  172.5 6.5 %slice-start.1 = ((s8[7340032]{0:T(1024)(128)(4,1)}), s8[3145728]{0:T(1024)(128)(4,1)S(1)}, s32[]{:S(2)}) async-start(s8[7340032]{0:T(1024)(128)(4,1)} %bitcast.114), calls=%async_computation.7 | async-start | bytes 6291456
  213.0 11.8 %all-to-all-start.1 = ((f32[4,64,256]{2,1,0:T(8,128)}), f32[4,64,256]{2,1,0:T(8,128)S(1)}, u32[]{:S(2)}, u32[]{:S(2)}) async-start(f32[4,64,256]{2,1,0:T(8,128)} %broadcast_in_dim.21), calls=%async_computation.1 | async-start | bytes 524288 | tf_op jit(solution)/shard_map/all_to_all | solution.py:33
  218.3 105.2 %all-gather.7.cloned.1.call-start = ((), (), s32[]{:S(2)}) async-start(), calls=%async_computation.4 | async-start | bytes 1310720 | tf_op jit(solution)/shard_map/all_gather | solution.py:86
  293.2 12.4 %copy-start.2 = (f32[64,256]{1,0:T(8,128)}, f32[64,256]{1,0:T(8,128)S(1)}, u32[]{:S(2)}) copy-start(f32[64,256]{1,0:T(8,128)S(1)} %fusion.153) | copy-start | bytes 196612
Sparse Core Ops, SparseCore 0:
  11.0 51.8 all-gather.8
  66.8 95.0 all-reduce.2
  168.3 61.9 all-gather.4
  303.5 20.0 all-gather.6
where the time goes:
time: 339 us
  waiting for transfers between devices  175 us (52%)
  other arithmetic  61.4 us (18%)
  blocking collectives  36 us (11%)
  matrix products  35.1 us (10%)
  between operations  15.3 us (5%)
  local copies, waits for them, and re-layouts  10.1 us (3%)
  starting transfers between devices  5.42 us (2%)
    psum x1, waiting for transfers between devices, body(): gram_sums = lax.psum(partial_value, 'tok')  94.8 us
    all_gather x2, waiting for transfers between devices, broadcast(): lax.all_gather(array, axis)  59.5 us
    another operation x6, other arithmetic, body(): factor = jnp.linalg.cholesky(diagonal_part)  34 us
    all_to_all x1, blocking collectives, summed_on_arrival(): tiles = lax.all_to_all(in_blocks(array, dim, peers), axis, 0, 0, tiled=True)  25.9 us
    another operation x4, other arithmetic, body(): lax.linalg.triangular_solve(factor, whole_right, left_side=True, lower=True)  19.7 us
    dot_general x16, matrix products, body(): jnp.einsum('mip,mio->po', gram_part, weight_part, preferred_element_type=...  17.8 us
    all_gather x1, waiting for transfers between devices, body(): lax.all_gather(solved_columns, 'row', axis=0, tiled=True)  14.3 us
    all_gather x1, blocking collectives, body(): solved_columns = lax.all_gather(solved, 'col', axis=1, tiled=True)  10.1 us
  transfers between devices with their start and end apart: 5, of which 5 were waited for; matrix products, arithmetic and copies ran while one was open for 7% of the time, Pallas kernels for 0%

commit v1 on v0

--- a/solution.py
+++ b/solution.py
@@ -52,7 +52,8 @@
     partial_value = jnp.einsum(
         "mti,mtp->mip", activations, panel_tokens, preferred_element_type=jnp.float32
     )
-    gram_sums = lax.psum(partial_value, "tok")
+    blocks = lax.all_gather(partial_value, "tok", axis=0, tiled=False)
+    gram_sums = blocks.sum(axis=0)
     row_ids = first_row + jnp.arange(rows_here, dtype=jnp.int32)[:, None]
     col_ids = jnp.arange(panel_width, dtype=jnp.int32)[None, :]
     on_diagonal = row_ids == col_ids

time: 339 us -> 550 us (1.62)
  waiting for transfers between devices: 175 us -> 373 us
  other arithmetic: 61.4 us -> 73.9 us
    all_gather x0 -> x1, waiting for transfers between devices: none -> 287 us  [body(): blocks = lax.all_gather(partial_value, 'tok', axis=0, tiled=False)]
    psum x1 -> x0, waiting for transfers between devices: 94.8 us -> none  [body(): gram_sums = lax.psum(partial_value, 'tok')]
    reduce_sum x0 -> x1, other arithmetic: none -> 12.8 us  [body(): gram_sums = blocks.sum(axis=0)]
  transfers between devices with their start and end apart: 5 -> 5, of which waited for: 5 -> 5; matrix products, arithmetic and copies ran while one was open for 7% -> 4% of each run, Pallas kernels for 0% -> 0%
where the time goes in v1:
time: 550 us; the launch traced here: 549 us
  waiting for transfers between devices  373 us (68%)
  other arithmetic  73.9 us (13%)
  blocking collectives  35.4 us (6%)
  matrix products  31.7 us (6%)
  local copies, waits for them, and re-layouts  15.3 us (3%)
  between operations  15.2 us (3%)
    all_gather x1, waiting for transfers between devices, body(): blocks = lax.all_gather(partial_value, 'tok', axis=0, tiled=False)  287 us
    all_gather x2, waiting for transfers between devices, broadcast(): lax.all_gather(array, axis)  62.3 us
    another operation x6, other arithmetic, body(): factor = jnp.linalg.cholesky(diagonal_part)  34 us
    all_to_all x1, blocking collectives, summed_on_arrival(): tiles = lax.all_to_all(in_blocks(array, dim, peers), axis, 0, 0, tiled=True)  25.3 us
    another operation x4, other arithmetic, body(): lax.linalg.triangular_solve(factor, whole_right, left_side=True, lower=True)  19.7 us
    all_gather x1, waiting for transfers between devices, body(): lax.all_gather(solved_columns, 'row', axis=0, tiled=True)  17.3 us
    dot_general x16, matrix products, body(): jnp.einsum('mip,mio->po', gram_part, weight_part, preferred_element_type=...  15 us
    reduce_sum x1, other arithmetic, body(): gram_sums = blocks.sum(axis=0)  12.8 us
  transfers between devices with their start and end apart: 5, of which 5 were waited for; matrix products, arithmetic and copies ran while one was open for 4% of the time, Pallas kernels for 0%

profile of v1, /device:TPU:1, one launch (start us, length us, event | category | flops | bytes accessed | tf_op | source)
XLA Modules:
  0.0 549.1 jit_solution(9039926788433031201)
XLA Ops:
  7.2 1.6 slice.77
  8.9 54.1 %all-gather.11.cloned.1.call-done = bf16[32,128,256]{2,1,0:T(8,128)(2,1)} async-done(((bf16[2,128,256]{2,1,0:T(8,128)(2,1)}), bf16[32,128,256]{2,1,0:T(8,128)(2,1)}) %all-gather.11.cloned.1.call-update) | async-done | bytes 2097168 | tf_op jit(solution)/shard_map/all_gather | solution.py:10
  62.9 3.7 fusion.151
  66.8 286.6 %all-gather.13.cloned.1.call-done = f32[16,1792,256]{2,1,0:T(8,128)} async-done(((f32[2,1792,256]{2,1,0:T(8,128)}), f32[16,1792,256]{2,1,0:T(8,128)}) %all-gather.13.cloned.1.call-update) | async-done | bytes 29360144 | tf_op jit(solution)/shard_map/all_gather | solution.py:55
  353.5 12.8 %reduce_sum.18 = f32[2,1792,256]{2,1,0:T(8,128)} reduce(f32[8,2,1792,256]{3,2,1,0:T(8,128)} %bitcast.112, f32[]{:T(128)} %constant.833.clone.1), dimensions={0}, to_apply=%region_0.1 | reduce | flops 6422528 | bytes 33030148 | tf_op jit(solution)/shard_map/reduce_sum | solution.py:56
  366.3 5.2 copy.7
  371.5 3.7 fusion.163
  375.4 1.7 copy-done
  378.0 2.1 fusion.39
  380.1 1.9 fusion.63
  382.1 2.1 fusion.87
  384.2 1.9 fusion.111
  386.1 2.0 fusion.45
  393.1 25.3 %all_to_all.10 = f32[16,64,256]{2,1,0:T(8,128)S(1)} all-to-all(f32[16,64,256]{2,1,0:T(8,128)S(1)} %bitcast.113), channel_id=1, replica_groups=mesh['tok'=8,'row'=4,'col'=4] {'row','col'}, dimensions={0} | all-to-all | bytes 2097152 | tf_op jit(solution)/shard_map/all_to_all | solution.py:21
  419.2 4.2 all-to-all-start.1
  423.4 6.8 %all-to-all-done.1 = f32[4,64,256]{2,1,0:T(8,128)S(1)} async-done(((f32[4,64,256]{2,1,0:T(8,128)}), f32[4,64,256]{2,1,0:T(8,128)S(1)}, u32[]{:S(2)}, u32[]{:S(2)}) %all-to-all-start.1) | async-done | bytes 262176 | tf_op jit(solution)/shard_map/all_to_all | solution.py:33
  430.2 8.2 %all-gather.7.cloned.1.call-done = f32[16,256,256]{2,1,0:T(8,128)} async-done(((f32[1,256,256]{2,1,0:T(8,128)}), f32[16,256,256]{2,1,0:T(8,128)}) %all-gather.7.cloned.1.call-update) | async-done | bytes 4194320 | tf_op jit(solution)/shard_map/all_gather | solution.py:10
  438.4 1.0 dynamic_slice.70
  439.5 1.0 fusion.150
  440.5 11.7 %cholesky.50 = f32[128,128]{1,0:T(8,128)S(1)} custom-call(f32[128,128]{1,0:T(8,128)S(1)} %cholesky.118), custom_call_target="Cholesky" | custom-call | tf_op jit(solution)/shard_map/jit(cholesky)/cholesky | solution.py:76
  452.3 9.8 %custom-call.16 = f32[1,128,128]{1,2,0:T(8,128)S(1)} custom-call(f32[1,128,128]{2,1,0:T(8,128)S(1)} %get-tuple-element.27), custom_call_target="InvertDiagBlocksLowerTriangular" | custom-call | tf_op jit(solution)/shard_map/jit(cholesky)/cholesky | solution.py:76
  462.6 11.7 %cholesky.105 = f32[128,128]{1,0:T(8,128)S(1)} custom-call(f32[128,128]{1,0:T(8,128)S(1)} %convolution_subtract_fusion.2), custom_call_target="Cholesky" | custom-call | tf_op jit(solution)/shard_map/jit(cholesky)/cholesky | solution.py:76
  476.4 4.2 while.1
  477.3 1.3 bitcast_dynamic-update-slice_fusion.2
  479.3 1.3 bitcast_dynamic-update-slice_fusion.2
  480.7 19.7 %custom-call.17 = f32[2,128,128]{1,2,0:T(8,128)S(1)} custom-call(f32[2,128,128]{2,1,0:T(8,128)S(1)} %get-tuple-element.9), custom_call_target="InvertDiagBlocksLowerTriangular" | custom-call | tf_op jit(solution)/shard_map/triangular_solve | solution.py:82
  501.3 10.1 %all_gather.27 = f32[64,1024]{1,0:T(8,128)} all-gather(f32[64,256]{1,0:T(8,128)S(1)} %fusion.153), channel_id=1, replica_groups=mesh['tok'=8,'row'=4,'col'=4] {'col'}, dimensions={1}, use_global_device_ids=true | all-gather | bytes 327680 | tf_op jit(solution)/shard_map/all_gather | solution.py:84
  511.4 2.2 fusion.175
  513.7 1.0 fusion.132
  514.7 1.0 convolution_subtract_fusion
  516.6 17.3 %all-gather.9.cloned.1.call-done = f32[256,1024]{1,0:T(8,128)} async-done(((f32[64,1024]{1,0:T(8,128)}), f32[256,1024]{1,0:T(8,128)}) %all-gather.9.cloned.1.call-update) | async-done | bytes 1048592 | tf_op jit(solution)/shard_map/all_gather | solution.py:87
  533.9 8.7 %convolution_convert_fusion = bf16[1792,1024]{1,0:T(8,128)(2,1)} fusion(f32[256,1024]{1,0:T(8,128)} %all-gather.9.cloned.1.call-done, f32[1792,128]{0,1:T(8,128)S(1)} %fusion.158, f32[1792,128]{0,1:T(8,128)S(1)} %fusion.132), kind=kOutput, calls=%fused_computation.2 | convolution fusion | flops 5639438336 | bytes 6553600 | tf_op jit(solution)/shard_map/dot_general | solution.py:85
  (58 shorter events, 11.9 us)
Async XLA Ops:
  7.2 55.7 %all-gather.11.cloned.1.call-start = ((), (), s32[]{:S(2)}) async-start(), calls=%async_computation.4 | async-start | bytes 2228224 | tf_op jit(solution)/shard_map/all_gather | solution.py:10
  8.8 344.7 %all-gather.13.cloned.1.call-start = ((), (), s32[]{:S(2)}) async-start(), calls=%async_computation.5 | async-start | bytes 33030144 | tf_op jit(solution)/shard_map/all_gather | solution.py:55
  66.6 371.8 %all-gather.7.cloned.1.call-start = ((), (), s32[]{:S(2)}) async-start(), calls=%async_computation.2 | async-start | bytes 4456448 | tf_op jit(solution)/shard_map/all_gather | solution.py:10
  375.2 1.9 copy-start
  375.2 2.8 copy-start.1
  378.0 10.1 %slice-start = ((s8[7340032]{0:T(1024)(128)(4,1)}), s8[4194304]{0:T(1024)(128)(4,1)S(1)}, s32[]{:S(2)}) async-start(s8[7340032]{0:T(1024)(128)(4,1)} %bitcast.116), calls=%async_computation.6 | async-start | bytes 8388608
  382.1 6.1 %slice-start.1 = ((s8[7340032]{0:T(1024)(128)(4,1)}), s8[3145728]{0:T(1024)(128)(4,1)S(1)}, s32[]{:S(2)}) async-start(s8[7340032]{0:T(1024)(128)(4,1)} %bitcast.116), calls=%async_computation.7 | async-start | bytes 6291456
  419.2 11.0 %all-to-all-start.1 = ((f32[4,64,256]{2,1,0:T(8,128)}), f32[4,64,256]{2,1,0:T(8,128)S(1)}, u32[]{:S(2)}, u32[]{:S(2)}) async-start(f32[4,64,256]{2,1,0:T(8,128)} %broadcast_in_dim.21), calls=%async_computation.1 | async-start | bytes 524288 | tf_op jit(solution)/shard_map/all_to_all | solution.py:33
  423.4 110.5 %all-gather.9.cloned.1.call-start = ((), (), s32[]{:S(2)}) async-start(), calls=%async_computation.3 | async-start | bytes 1310720 | tf_op jit(solution)/shard_map/all_gather | solution.py:87
  501.3 12.4 %copy-start.2 = (f32[64,256]{1,0:T(8,128)}, f32[64,256]{1,0:T(8,128)S(1)}, u32[]{:S(2)}) copy-start(f32[64,256]{1,0:T(8,128)S(1)} %fusion.153) | copy-start | bytes 196612
Sparse Core Ops, SparseCore 0:
  11.0 51.8 all-gather.10
  66.8 286.6 all-gather.12
  378.1 60.3 all-gather.6
  511.6 22.2 all-gather.8
